TPU v7x, 32 devices: a whole 2x2x4 slice. The times are simulated.
32 devices in a mesh: attn: 4 (over y, x), expert: 8 (over z, core).
Axes of the slice: x: 2, y: 2, z: 4, core: 2. Of those that a mesh axis runs over, the one named last changes fastest.
Arguments:
- tokens: bfloat16 [1024, 2880], P(('attn', 'expert')), may hold values from -6 to 6
- expert_ids: int32 [1024, 4], P(('attn', 'expert')), may hold values from 0 to 7, all different within a row; in each aligned block of 32 rows (0 to 31, 32 to 63, ...) at most 32 rows name the same one
- gate_probs: float32 [1024, 4], P(('attn', 'expert')), may hold values from 0.05 to 0.6
- shed_blocks: int32 [8], replicated, may hold values from 0 to 4, as said below
- partner: int32 [8], replicated, may hold values from 0 to 7, as said below
- gate_weight: bfloat16 [8, 2880, 2880], P('expert', None, 'attn'), may hold values from -0.109375 to 0.109375
- up_weight: bfloat16 [8, 2880, 2880], P('expert', None, 'attn'), may hold values from -0.109375 to 0.109375
- down_weight: bfloat16 [8, 2880, 2880], P('expert', 'attn'), may hold values from -0.109375 to 0.109375
Outputs:
- moe_out: bfloat16 [1024, 2880], P(('attn', 'expert'))
Inputs may be any that keep to these rules, and one draw needn't show every extreme that they name: `expert_ids`: in the rows of one device, no expert is named by more than 32 rows; the 4 experts of a token differ. `shed_blocks`: some expert has exactly 4. partner pairs the experts: partner[partner[e]] = e and partner[e] != e.
All inputs are finite; a program needn't handle non-finite values.
Results may differ from a plain program's by a relative error of at most 0.0081.
Values may be sent and summed in bfloat16 or wider, within the bound.
A program may use at most 128 MiB of HBM per device.

v0:
```python
import jax
import jax.numpy as jnp
from jax import lax
from jax.experimental import pallas as pl
from jax.experimental.pallas import tpu as pltpu
from jax.sharding import PartitionSpec as P

SHED_MOST = 4


SWISH_SCALE = 1.702
LANES = 128
VMEM_BYTES = 60 * 2**20
MESH = pl.DeviceIdType.MESH

OWN_X, OWN_Y, OWN_C, FWD_Y, FWD_X, PASS_X, PASS_Y, PASS_D = range(8)
SUM_C, HALF_X, HALF_Y, FULL_X, FULL_Y, BACK_Z, OUT_Z = range(8, 15)
META_Z, META_A, META_C = range(15, 18)
KINDS = 18


def lookup(table, indices):
    places = jnp.arange(table.shape[0], dtype=jnp.int32)
    return jnp.sum(jnp.where(indices[:, None] == places[None, :], table[None, :], 0), axis=1)


def served_rows(shed_blocks, partner, capacity):
    me = lax.axis_index("expert").astype(jnp.int32)[None]
    other = lookup(partner, me)
    block_size = capacity // 8
    return capacity + block_size * (lookup(shed_blocks, me) - lookup(shed_blocks, other))


def activate(gate_part, up_part, weight):
    return (gate_part * jax.nn.sigmoid(SWISH_SCALE * gate_part) * (up_part + 1.0) * weight).astype(
        jnp.bfloat16
    )


def kernel(
    tokens,
    ids,
    probs,
    shed,
    partner,
    gate_hbm,
    up_hbm,
    down_hbm,
    out,
    x,
    meta,
    m,
    wcol,
    part,
    core_in,
    total,
    half_in,
    full_in,
    z_out,
    z_in,
    kept,
    gate,
    up,
    down,
    hidden,
    send_sem,
    recv_sem,
    load_sem,
):
    planes = x.shape[0]
    rows, width = tokens.shape
    half = rows // 2
    top = ids.shape[0]
    capacity = rows * top * x.shape[2]
    a = lax.axis_index("attn")
    e = lax.axis_index("expert")
    z, c = e // 2, e % 2

    def xor(value, bits):
        result = value
        for bit in (1, 2, 4, 8):
            if bits & bit:
                result = result + bit - 2 * bit * ((value // bit) % 2)
        return result

    xn, yn, dn = xor(a, 1), xor(a, 2), xor(a, 3)
    oc = 1 - c
    to_x, to_y, to_d, to_c = (xn, e), (yn, e), (dn, e), (a, z * 2 + oc)

    def plane(s):
        low = (z % 2 + s % 2) % 2
        high = (z // 2 + s // 2) % 2
        return high * 2 + low

    def copy(kind, s, src, dst, to):
        return pltpu.make_async_remote_copy(
            src_ref=src,
            dst_ref=dst,
            send_sem=send_sem.at[kind, s],
            recv_sem=recv_sem.at[kind, s],
            device_id=to,
            device_id_type=MESH,
        )

    def same(kind, s, ref, to):
        return copy(kind, s, ref, ref, to)

    lo, hi = pl.ds(0, half), pl.ds(half, half)

    def make(kind, s):
        p = plane(s)
        if kind == OUT_Z:
            return copy(kind, s, tokens, x.at[z, c, a], (a, p * 2 + c))
        if kind == OWN_X:
            return same(kind, s, x.at[p, c, a], to_x)
        if kind == OWN_Y:
            return same(kind, s, x.at[p, c, a], to_y)
        if kind == OWN_C:
            return same(kind, s, x.at[p, c, a], to_c)
        if kind == FWD_Y:
            return same(kind, s, x.at[p, c, xn, lo], to_y)
        if kind == FWD_X:
            return same(kind, s, x.at[p, c, yn, hi], to_x)
        if kind == PASS_X:
            return same(kind, s, x.at[p, c, xn], to_c)
        if kind == PASS_Y:
            return same(kind, s, x.at[p, c, yn], to_c)
        if kind == PASS_D:
            return same(kind, s, x.at[p, c, dn], to_c)
        if kind == SUM_C:
            return copy(kind, s, part.at[s, oc], core_in.at[s], to_c)
        if kind == HALF_X:
            return copy(kind, s, total.at[s, dn, lo], half_in.at[s, 0], to_x)
        if kind == HALF_Y:
            return copy(kind, s, total.at[s, dn, hi], half_in.at[s, 1], to_y)
        if kind == FULL_X:
            return copy(kind, s, total.at[s, xn], full_in.at[s, 0], to_x)
        if kind == FULL_Y:
            return copy(kind, s, total.at[s, yn], full_in.at[s, 1], to_y)
        if kind == BACK_Z:
            return copy(kind, s, z_out.at[s], z_in.at[s], (a, p * 2 + c))
        if kind == META_Z:
            return copy(kind, s, meta, m.at[a, z, c], (a, p * 2 + c))
        if kind == META_A:
            to = (to_x, to_x, to_y, to_d)[s]
            return same(kind, s, m.at[a, :, c], to)
        if kind == META_C:
            return same(kind, s, m.at[:, :, c], to_c)

    def start(s, *kinds):
        for kind in kinds:
            make(kind, s).start()

    def arrived(s, *kinds):
        for kind in kinds:
            make(kind, s).wait_recv()

    def sent(s, *kinds):
        for kind in kinds:
            make(kind, s).wait_send()

    def widen(ref):
        return ref[...].astype(jnp.float32)

    barrier = pltpu.get_barrier_semaphore()
    peers = [to_x, to_y, to_d, to_c] + [(a, plane(s) * 2 + c) for s in range(1, planes)]
    for peer in peers:
        pl.semaphore_signal(barrier, inc=1, device_id=peer, device_id_type=MESH)

    own = pltpu.make_async_copy(tokens, x.at[z, c, a], load_sem.at[3])
    own_meta = pltpu.make_async_copy(meta, m.at[a, z, c], load_sem.at[4])
    loads = [
        pltpu.make_async_copy(gate_hbm.at[0], gate, load_sem.at[0]),
        pltpu.make_async_copy(up_hbm.at[0], up, load_sem.at[1]),
        pltpu.make_async_copy(down_hbm.at[0], down, load_sem.at[2]),
    ]
    own.start()
    meta[...] = jnp.full(meta.shape, -1.0, jnp.float32)
    meta[:top, :rows] = ids[...].astype(jnp.float32)
    meta[top:, :rows] = probs[...]
    for load in loads:
        load.start()
    pl.semaphore_wait(barrier, len(peers))

    for s in range(1, planes):
        start(s, META_Z)
    own_meta.start()
    own.wait()
    start(0, OWN_X, OWN_Y, OWN_C)
    for s in range(1, planes):
        start(s, OUT_Z)
    own_meta.wait()

    def stage_own(s):
        arrived(s, OUT_Z)
        start(s, OWN_X, OWN_Y, OWN_C)

    def stage_forward(s):
        arrived(s, OWN_X)
        start(s, FWD_Y, PASS_X)
        arrived(s, OWN_Y)
        start(s, FWD_X, PASS_Y)

    for s in range(1, planes):
        arrived(s, META_Z)
    for s in range(1, 4):
        start(s, META_A)
    stage_forward(0)
    for s in range(1, 4):
        arrived(s, META_A)
    start(0, META_C)
    stage_own(1)
    stage_own(2)
    arrived(0, META_C)

    def row_weights():
        table = m[...].reshape(m.shape[0] * m.shape[1] * m.shape[2], 2 * top, LANES)
        blocks = table.shape[0]
        named = table[:, :top, :] == e.astype(jnp.float32)
        mask = jnp.sum(jnp.where(named, 1.0, 0.0), axis=1)
        prob = jnp.sum(jnp.where(named, table[:, top:, :], 0.0), axis=1)
        mask16 = mask.astype(jnp.bfloat16)
        i = lax.broadcasted_iota(jnp.int32, (LANES, LANES), 0)
        j = lax.broadcasted_iota(jnp.int32, (LANES, LANES), 1)
        before = jnp.where(i < j, 1.0, 0.0).astype(jnp.bfloat16)
        inside = jnp.dot(mask16, before, preferred_element_type=jnp.float32)
        i = lax.broadcasted_iota(jnp.int32, (blocks, blocks), 0)
        j = lax.broadcasted_iota(jnp.int32, (blocks, blocks), 1)
        earlier = jnp.where(j < i, 1.0, 0.0).astype(jnp.bfloat16)
        ahead = jnp.dot(earlier, mask16, preferred_element_type=jnp.float32)
        rank = inside + jnp.sum(ahead, axis=1, keepdims=True)
        bound = capacity + capacity // 8 * (shed[e] - shed[partner[e]])
        weight = jnp.where(rank < bound.astype(jnp.float32), prob, 0.0)
        i = lax.broadcasted_iota(jnp.int32, (rows, LANES), 0)
        j = lax.broadcasted_iota(jnp.int32, (rows, LANES), 1)
        for aa in range(m.shape[0]):
            for zz in range(m.shape[1]):
                for cc in range(2):
                    block = (aa * m.shape[1] + zz) * 2 + cc
                    spread = jnp.where(i == j, weight[block : block + 1, :], 0.0)
                    wcol[zz, cc, aa] = jnp.sum(spread, axis=1, keepdims=True)

    row_weights()
    for load in loads:
        load.wait()
    stage_forward(1)

    count = 2 * x.shape[2] * rows
    along = (((1,), (1,)), ((), ()))

    def compute_hidden(s):
        p = plane(s)
        xs = x[p].reshape(count, width)
        gate_part = lax.dot_general(xs, gate[...], along, preferred_element_type=jnp.float32)
        up_part = lax.dot_general(xs, up[...], along, preferred_element_type=jnp.float32)
        hidden[...] = activate(gate_part, up_part, wcol[p].reshape(count, 1))

    def compute_share(s):
        step = 8 * LANES
        for first in range(0, width, step):
            cols = slice(first, min(first + step, width))
            share = jnp.dot(hidden[...], down[:, cols], preferred_element_type=jnp.float32)
            part[s, :, :, :, cols] = share.astype(jnp.bfloat16).reshape(
                2, x.shape[2], rows, cols.stop - cols.start
            )

    def order(t):
        return (t + 1) % planes

    def body(t, carry):
        @pl.when(t < planes)
        def _():
            s = order(t)
            arrived(s, FWD_Y, FWD_X)
            start(s, PASS_D)
            arrived(s, OWN_C, PASS_X, PASS_Y, PASS_D)

        @pl.when(t + 3 < planes)
        def _():
            stage_own(t + 3)

        @pl.when(t < planes)
        def _():
            compute_hidden(order(t))

        @pl.when(t + 2 < planes)
        def _():
            stage_forward(t + 2)

        @pl.when(jnp.logical_and(t >= 1, t < planes + 1))
        def _():
            s = order(t - 1)
            arrived(s, HALF_X, HALF_Y)
            low = widen(total.at[s, yn, lo]) + widen(half_in.at[s, 0])
            total[s, yn, lo] = low.astype(jnp.bfloat16)
            start(s, FULL_Y)
            high = widen(total.at[s, xn, hi]) + widen(half_in.at[s, 1])
            total[s, xn, hi] = high.astype(jnp.bfloat16)
            start(s, FULL_X)

        @pl.when(t < planes)
        def _():
            s = order(t)
            compute_share(s)
            start(s, SUM_C)
            arrived(s, SUM_C)
            total[s] = (widen(part.at[s, c]) + widen(core_in.at[s])).astype(jnp.bfloat16)
            start(s, HALF_X, HALF_Y)

        @pl.when(t >= 2)
        def _():
            s = order(t - 2)
            arrived(s, FULL_X, FULL_Y)
            value = widen(total.at[s, a]) + widen(full_in.at[s, 0]) + widen(full_in.at[s, 1])

            @pl.when(s == 0)
            def _():
                kept[...] = value

            @pl.when(s > 0)
            def _():
                z_out[s] = value.astype(jnp.bfloat16)
                start(s, BACK_Z)

        return carry

    lax.fori_loop(0, planes + 2, body, 0)

    value = kept[...]
    for s in range(1, planes):
        arrived(s, BACK_Z)
        value = value + widen(z_in.at[s])
    out[...] = value.astype(out.dtype)

    def drain(s, carry):
        sent(s, *range(OWN_X, BACK_Z))

        @pl.when(s > 0)
        def _():
            sent(s, BACK_Z, OUT_Z, META_Z)

        return carry

    lax.fori_loop(0, planes, drain, 0)
    for s in range(1, 4):
        sent(s, META_A)
    sent(0, META_C)


def fused_bytes(group_count, planes, rows, width, hidden):
    wide = -(-width // LANES) * LANES
    block = rows * wide * 2
    weights = 2 * width * (-(-hidden // LANES) * LANES) * 2 + hidden * wide * 2
    return weights + planes * group_count * block * (2 + 2 + 1 + 1 + 2) + 12 * 2**20


def fused(tokens, ids, probs, shed, partner, gate_weight, up_weight, down_weight, group_count, planes):
    rows, width = tokens.shape
    hidden = gate_weight.shape[1]
    count = 2 * group_count * rows
    table = (2 * ids.shape[0], LANES)
    bf16, f32 = jnp.bfloat16, jnp.float32
    vmem = pl.BlockSpec(memory_space=pltpu.VMEM)
    smem = pl.BlockSpec(memory_space=pltpu.SMEM)
    hbm = pl.BlockSpec(memory_space=pl.ANY)
    return pl.pallas_call(
        kernel,
        out_shape=jax.ShapeDtypeStruct((rows, width), bf16),
        in_specs=[vmem, vmem, vmem, smem, smem, hbm, hbm, hbm],
        out_specs=vmem,
        scratch_shapes=[
            pltpu.VMEM((planes, 2, group_count, rows, width), bf16),
            pltpu.VMEM(table, f32),
            pltpu.VMEM((group_count, planes, 2) + table, f32),
            pltpu.VMEM((planes, 2, group_count, rows, 1), f32),
            pltpu.VMEM((planes, 2, group_count, rows, width), bf16),
            pltpu.VMEM((planes, group_count, rows, width), bf16),
            pltpu.VMEM((planes, group_count, rows, width), bf16),
            pltpu.VMEM((planes, 2, rows // 2, width), bf16),
            pltpu.VMEM((planes, 2, rows, width), bf16),
            pltpu.VMEM((planes, rows, width), bf16),
            pltpu.VMEM((planes, rows, width), bf16),
            pltpu.VMEM((rows, width), f32),
            pltpu.VMEM((hidden, width), bf16),
            pltpu.VMEM((hidden, width), bf16),
            pltpu.VMEM((hidden, width), bf16),
            pltpu.VMEM((count, hidden), bf16),
            pltpu.SemaphoreType.DMA((KINDS, planes)),
            pltpu.SemaphoreType.DMA((KINDS, planes)),
            pltpu.SemaphoreType.DMA((5,)),
        ],
        compiler_params=pltpu.CompilerParams(
            collective_id=0, has_side_effects=True, vmem_limit_bytes=VMEM_BYTES
        ),
    )(tokens, ids, probs, shed, partner, gate_weight, up_weight, down_weight)


def gathered(tokens, expert_ids, gate_probs, bound, gate_weight, up_weight, down_weight):
    both = ("attn", "expert")
    all_ids = lax.all_gather(expert_ids, both, axis=0, tiled=True)
    all_probs = lax.all_gather(gate_probs, both, axis=0, tiled=True)
    rows = lax.all_gather(tokens, both, axis=0, tiled=True)
    named = all_ids == lax.axis_index("expert").astype(jnp.int32)
    mask = jnp.any(named, axis=1).astype(jnp.int32)
    rank = jnp.cumsum(mask) - mask
    weight = jnp.sum(jnp.where(named, all_probs, 0.0), axis=1)
    weight = jnp.where(rank < bound, weight, 0.0)
    gate_part = jnp.dot(rows, gate_weight[0], preferred_element_type=jnp.float32)
    up_part = jnp.dot(rows, up_weight[0], preferred_element_type=jnp.float32)
    hidden = activate(gate_part, up_part, weight[:, None])
    share = jnp.dot(hidden, down_weight[0], preferred_element_type=jnp.float32).astype(jnp.bfloat16)
    share = lax.psum_scatter(share, "attn", scatter_dimension=0, tiled=True)
    return lax.psum_scatter(share, "expert", scatter_dimension=0, tiled=True)


def on_device(
    tokens, expert_ids, gate_probs, shed_blocks, partner, gate_weight, up_weight, down_weight
):
    rows, width = tokens.shape
    group_count, expert_count = lax.axis_size("attn"), lax.axis_size("expert")
    top_count = expert_ids.shape[1]
    planes = expert_count // 2
    fits = fused_bytes(group_count, planes, rows, width, gate_weight.shape[2]) <= VMEM_BYTES
    if group_count != 4 or planes != 4 or rows % 32 or rows > LANES or not fits:
        bound = served_rows(shed_blocks, partner, rows * top_count * group_count)
        return gathered(
            tokens, expert_ids, gate_probs, bound, gate_weight, up_weight, down_weight
        )
    return fused(
        tokens,
        expert_ids.T,
        gate_probs.T,
        shed_blocks,
        partner,
        jnp.swapaxes(gate_weight, 1, 2),
        jnp.swapaxes(up_weight, 1, 2),
        down_weight,
        group_count,
        planes,
    )


def solution(mesh):
    in_specs = (
        P(("attn", "expert"), None),
        P(("attn", "expert"), None),
        P(("attn", "expert"), None),
        P(),
        P(),
        P("expert", None, "attn"),
        P("expert", None, "attn"),
        P("expert", "attn", None),
    )
    out_specs = P(("attn", "expert"), None)
    return jax.shard_map(
        on_device, mesh=mesh, in_specs=in_specs, out_specs=out_specs, check_vma=False
    )
```

profile of v0, /device:TPU:9, one launch (start us, length us, event | category | flops | bytes accessed | tf_op | source)
XLA Modules:
  0.0 77.8 jit_solution(13792382818791526783)
XLA Ops:
  0.0 76.1 %shard_map.82 = bf16[32,2880]{1,0:T(8,128)(2,1)} custom-call(bf16[32,2880]{1,0:T(8,128)(2,1)} %tokens.1, s32[4,32]{1,0:T(4,128)} %bitcast.6, f32[4,32]{1,0:T(4,128)} %bitcast.7, s32[8]{0:T(128)} %shed.1, s32[8]{0:T(128)} %partner.1, bf16[1,720,2880]{2,1,0:T(8,128)(2,1)} %bitcast.4, bf16[1,720,2880]{2,1,0:T(8,128)(2,1)} %bitcast.5, bf16[1,720,2880]{2,1,0:T(8,128)(2,1)} %down_hbm.1), custom_call_target="tpu_custom_call" | custom-call | tf_op jit(solution)/shard_map/pallas_call | solution.py:366
  76.1 1.6 %copy.10 = bf16[32,2880]{1,0:T(8,128)(2,1)} copy(bf16[32,2880]{1,0:T(8,128)(2,1)} %shard_map.82) | data formatting | bytes 368640
where the time goes:
time: 77.9 us; the launch traced here: 77.8 us
  Pallas kernels  76.1 us (98%)
  local copies, waits for them, and re-layouts  1.61 us (2%)
    pallas_call x1, Pallas kernels, fused(): pl.pallas_call(kernel, out_shape=jax.ShapeDtypeStruct((rows, width), bf16...  76.1 us
    unnamed x1, local copies, waits for them, and re-layouts  1.61 us

commit v1 on v0

--- a/solution.py
+++ b/solution.py
@@ -13,10 +13,10 @@
 VMEM_BYTES = 60 * 2**20
 MESH = pl.DeviceIdType.MESH
 
-OWN_X, OWN_Y, OWN_C, FWD_Y, FWD_X, PASS_X, PASS_Y, PASS_D = range(8)
-SUM_C, HALF_X, HALF_Y, FULL_X, FULL_Y, BACK_Z, OUT_Z = range(8, 15)
-META_Z, META_A, META_C = range(15, 18)
-KINDS = 18
+OWN_XA, OWN_XB, OWN_YA, OWN_YB, OWN_C, FWD_Y, FWD_X, PASS_X, PASS_Y, PASS_D = range(10)
+SUM_C, HALF_X, HALF_Y, FULL_XA, FULL_XB, FULL_YA, FULL_YB, BACK_Z, OUT_Z = range(10, 19)
+META_Z, META_A, META_C = range(19, 22)
+KINDS = 22
 
 
 def lookup(table, indices):
@@ -75,6 +75,7 @@
     a = lax.axis_index("attn")
     e = lax.axis_index("expert")
     z, c = e // 2, e % 2
+    middle = (z + z // 2) % 2
 
     def xor(value, bits):
         result = value
@@ -109,12 +110,14 @@
 
     def make(kind, s):
         p = plane(s)
-        if kind == OUT_Z:
-            return copy(kind, s, tokens, x.at[z, c, a], (a, p * 2 + c))
-        if kind == OWN_X:
-            return same(kind, s, x.at[p, c, a], to_x)
-        if kind == OWN_Y:
-            return same(kind, s, x.at[p, c, a], to_y)
+        if kind == OWN_XA:
+            return same(kind, s, x.at[p, c, a, lo], to_x)
+        if kind == OWN_XB:
+            return same(kind, s, x.at[p, c, a, hi], to_x)
+        if kind == OWN_YA:
+            return same(kind, s, x.at[p, c, a, hi], to_y)
+        if kind == OWN_YB:
+            return same(kind, s, x.at[p, c, a, lo], to_y)
         if kind == OWN_C:
             return same(kind, s, x.at[p, c, a], to_c)
         if kind == FWD_Y:
@@ -133,10 +136,14 @@
             return copy(kind, s, total.at[s, dn, lo], half_in.at[s, 0], to_x)
         if kind == HALF_Y:
             return copy(kind, s, total.at[s, dn, hi], half_in.at[s, 1], to_y)
-        if kind == FULL_X:
-            return copy(kind, s, total.at[s, xn], full_in.at[s, 0], to_x)
-        if kind == FULL_Y:
-            return copy(kind, s, total.at[s, yn], full_in.at[s, 1], to_y)
+        if kind == FULL_XA:
+            return copy(kind, s, total.at[s, xn, lo], full_in.at[s, 0, lo], to_x)
+        if kind == FULL_XB:
+            return copy(kind, s, total.at[s, xn, hi], full_in.at[s, 0, hi], to_x)
+        if kind == FULL_YA:
+            return copy(kind, s, total.at[s, yn, hi], full_in.at[s, 1, hi], to_y)
+        if kind == FULL_YB:
+            return copy(kind, s, total.at[s, yn, lo], full_in.at[s, 1, lo], to_y)
         if kind == BACK_Z:
             return copy(kind, s, z_out.at[s], z_in.at[s], (a, p * 2 + c))
         if kind == META_Z:
@@ -147,6 +154,10 @@
         if kind == META_C:
             return same(kind, s, m.at[:, :, c], to_c)
 
+    def hop(block, target):
+        p = plane(block)
+        return same(OUT_Z, block ^ target, x.at[p, c, a], (a, plane(target) * 2 + c))
+
     def start(s, *kinds):
         for kind in kinds:
             make(kind, s).start()
@@ -161,6 +172,9 @@
 
     def widen(ref):
         return ref[...].astype(jnp.float32)
+
+    def at_middle(run):
+        pl.when(middle == 1)(run)
 
     barrier = pltpu.get_barrier_semaphore()
     peers = [to_x, to_y, to_d, to_c] + [(a, plane(s) * 2 + c) for s in range(1, planes)]
@@ -180,38 +194,79 @@
     meta[top:, :rows] = probs[...]
     for load in loads:
         load.start()
+    own.wait()
+    own_meta.start()
+    own_meta.wait()
     pl.semaphore_wait(barrier, len(peers))
+
+    def share_own(s):
+        start(s, OWN_XA, OWN_YA, OWN_XB, OWN_YB, OWN_C)
+
+    def forward(s):
+        arrived(s, OWN_XA)
+        start(s, FWD_Y)
+        arrived(s, OWN_YA)
+        start(s, FWD_X)
+
+    def pass_near(s):
+        arrived(s, OWN_XB)
+        start(s, PASS_X)
+        arrived(s, OWN_YB)
+        start(s, PASS_Y)
+
+    def pass_far(s):
+        arrived(s, FWD_Y, FWD_X)
+        start(s, PASS_D)
+
+    def ready(s):
+        arrived(s, OWN_C, PASS_X, PASS_Y, PASS_D)
+
+    def take(s):
+        hop(0, s).wait_recv()
+
+    def out_1():
+        take(1)
+
+        @at_middle
+        def _():
+            hop(1, 3).start()
+
+        share_own(1)
+
+        @at_middle
+        def _():
+            take(3)
+            hop(3, 1).start()
+
+    def out_2():
+        take(2)
+
+        @at_middle
+        def _():
+            hop(2, 1).start()
+
+        share_own(2)
+
+    def out_3():
+        @pl.when(middle == 0)
+        def _():
+            take(3)
+
+        share_own(3)
 
     for s in range(1, planes):
         start(s, META_Z)
-    own_meta.start()
-    own.wait()
-    start(0, OWN_X, OWN_Y, OWN_C)
-    for s in range(1, planes):
-        start(s, OUT_Z)
-    own_meta.wait()
-
-    def stage_own(s):
-        arrived(s, OUT_Z)
-        start(s, OWN_X, OWN_Y, OWN_C)
-
-    def stage_forward(s):
-        arrived(s, OWN_X)
-        start(s, FWD_Y, PASS_X)
-        arrived(s, OWN_Y)
-        start(s, FWD_X, PASS_Y)
-
+    hop(0, 1).start()
+
+    @at_middle
+    def _():
+        hop(0, 3).start()
+
+    share_own(0)
     for s in range(1, planes):
         arrived(s, META_Z)
     for s in range(1, 4):
         start(s, META_A)
-    stage_forward(0)
-    for s in range(1, 4):
-        arrived(s, META_A)
-    start(0, META_C)
-    stage_own(1)
-    stage_own(2)
-    arrived(0, META_C)
 
     def row_weights():
         table = m[...].reshape(m.shape[0] * m.shape[1] * m.shape[2], 2 * top, LANES)
@@ -240,108 +295,150 @@
                     spread = jnp.where(i == j, weight[block : block + 1, :], 0.0)
                     wcol[zz, cc, aa] = jnp.sum(spread, axis=1, keepdims=True)
 
-    row_weights()
-    for load in loads:
-        load.wait()
-    stage_forward(1)
-
     count = 2 * x.shape[2] * rows
     along = (((1,), (1,)), ((), ()))
-
-    def compute_hidden(s):
+    units = gate.shape[0]
+
+    def hidden_piece(s, cols):
         p = plane(s)
         xs = x[p].reshape(count, width)
-        gate_part = lax.dot_general(xs, gate[...], along, preferred_element_type=jnp.float32)
-        up_part = lax.dot_general(xs, up[...], along, preferred_element_type=jnp.float32)
-        hidden[...] = activate(gate_part, up_part, wcol[p].reshape(count, 1))
-
-    def compute_share(s):
-        step = 8 * LANES
-        for first in range(0, width, step):
-            cols = slice(first, min(first + step, width))
-            share = jnp.dot(hidden[...], down[:, cols], preferred_element_type=jnp.float32)
-            part[s, :, :, :, cols] = share.astype(jnp.bfloat16).reshape(
-                2, x.shape[2], rows, cols.stop - cols.start
-            )
-
-    def order(t):
-        return (t + 1) % planes
+        gate_part = lax.dot_general(xs, gate[cols], along, preferred_element_type=jnp.float32)
+        up_part = lax.dot_general(xs, up[cols], along, preferred_element_type=jnp.float32)
+        hidden[:, cols] = activate(gate_part, up_part, wcol[p].reshape(count, 1))
+
+    def share_piece(s, cols):
+        share = jnp.dot(hidden[...], down[:, cols], preferred_element_type=jnp.float32)
+        part[s, :, :, :, cols] = share.astype(jnp.bfloat16).reshape(
+            2, x.shape[2], rows, cols.stop - cols.start
+        )
+
+    def chunks(size, step):
+        return [slice(first, min(first + step, size)) for first in range(0, size, step)]
+
+    def core_sum(s, block, part_rows):
+        return widen(part.at[s, c, block, part_rows]) + widen(core_in.at[s, block, part_rows])
+
+    whole = pl.ds(0, rows)
+
+    def begin(s):
+        arrived(s, SUM_C)
+        total[s, dn] = core_sum(s, dn, whole).astype(jnp.bfloat16)
+        start(s, HALF_X, HALF_Y)
+        total[s, xn, lo] = core_sum(s, xn, lo).astype(jnp.bfloat16)
+        start(s, FULL_XA)
+        total[s, yn, hi] = core_sum(s, yn, hi).astype(jnp.bfloat16)
+        start(s, FULL_YA)
+
+    def merge(s):
+        arrived(s, HALF_X)
+        low = core_sum(s, yn, lo) + widen(half_in.at[s, 0])
+        total[s, yn, lo] = low.astype(jnp.bfloat16)
+        start(s, FULL_YB)
+        arrived(s, HALF_Y)
+        high = core_sum(s, xn, hi) + widen(half_in.at[s, 1])
+        total[s, xn, hi] = high.astype(jnp.bfloat16)
+        start(s, FULL_XB)
+
+    def finish(s):
+        value = core_sum(s, a, whole)
+        arrived(s, FULL_XA, FULL_YA, FULL_XB, FULL_YB)
+        value = value + widen(full_in.at[s, 0]) + widen(full_in.at[s, 1])
+        if s == 0:
+            return value
+        z_out[s] = value.astype(jnp.bfloat16)
+        start(s, BACK_Z)
+
+    def get_meta():
+        for s in range(1, 4):
+            arrived(s, META_A)
+        start(0, META_C)
+
+    def get_weights():
+        arrived(0, META_C)
+        row_weights()
+        for load in loads:
+            load.wait()
+
+    call = lambda run, s: lambda: run(s)
+    before = [
+        call(forward, 0), get_meta, out_1, call(pass_near, 0), call(pass_far, 0), get_weights,
+        call(ready, 0),
+    ]
+    for run in before:
+        run()
+    hooks = {
+        (0, 1): [call(forward, 1)],
+        (0, 4): [out_2],
+        (0, 5): [call(pass_near, 1)],
+        (1, 0): [call(pass_far, 1), call(ready, 1)],
+        (1, 1): [call(forward, 2)],
+        (1, 3): [out_3],
+        (1, 5): [call(pass_near, 2)],
+        (2, 0): [call(pass_far, 2), call(ready, 2)],
+        (2, 1): [call(forward, 3), call(begin, 1)],
+        (2, 5): [call(pass_near, 3)],
+        (3, 0): [call(pass_far, 3), call(begin, 2), call(ready, 3)],
+        (3, 4): [call(merge, 2)],
+    }
+
+    def hook(t, place):
+        for step in range(planes):
+            runs = hooks.get((step, place), [])
+
+            def run_all(runs=runs):
+                for run in runs:
+                    run()
+
+            if runs:
+                pl.when(t == step)(run_all)
 
     def body(t, carry):
-        @pl.when(t < planes)
-        def _():
-            s = order(t)
-            arrived(s, FWD_Y, FWD_X)
-            start(s, PASS_D)
-            arrived(s, OWN_C, PASS_X, PASS_Y, PASS_D)
-
-        @pl.when(t + 3 < planes)
-        def _():
-            stage_own(t + 3)
-
-        @pl.when(t < planes)
-        def _():
-            compute_hidden(order(t))
-
-        @pl.when(t + 2 < planes)
-        def _():
-            stage_forward(t + 2)
-
-        @pl.when(jnp.logical_and(t >= 1, t < planes + 1))
-        def _():
-            s = order(t - 1)
-            arrived(s, HALF_X, HALF_Y)
-            low = widen(total.at[s, yn, lo]) + widen(half_in.at[s, 0])
-            total[s, yn, lo] = low.astype(jnp.bfloat16)
-            start(s, FULL_Y)
-            high = widen(total.at[s, xn, hi]) + widen(half_in.at[s, 1])
-            total[s, xn, hi] = high.astype(jnp.bfloat16)
-            start(s, FULL_X)
-
-        @pl.when(t < planes)
-        def _():
-            s = order(t)
-            compute_share(s)
-            start(s, SUM_C)
-            arrived(s, SUM_C)
-            total[s] = (widen(part.at[s, c]) + widen(core_in.at[s])).astype(jnp.bfloat16)
-            start(s, HALF_X, HALF_Y)
-
-        @pl.when(t >= 2)
-        def _():
-            s = order(t - 2)
-            arrived(s, FULL_X, FULL_Y)
-            value = widen(total.at[s, a]) + widen(full_in.at[s, 0]) + widen(full_in.at[s, 1])
-
-            @pl.when(s == 0)
-            def _():
-                kept[...] = value
-
-            @pl.when(s > 0)
-            def _():
-                z_out[s] = value.astype(jnp.bfloat16)
-                start(s, BACK_Z)
-
+        place = 0
+        for cols in chunks(units, 2 * LANES):
+            hook(t, place)
+            hidden_piece(t, cols)
+            place += 1
+        for cols in chunks(width, 8 * LANES):
+            hook(t, place)
+            share_piece(t, cols)
+            place += 1
+        start(t, SUM_C)
         return carry
 
-    lax.fori_loop(0, planes + 2, body, 0)
-
-    value = kept[...]
-    for s in range(1, planes):
+    lax.fori_loop(0, planes, body, 0)
+    begin(3)
+    merge(3)
+    merge(1)
+    begin(0)
+    finish(2)
+    finish(3)
+    merge(0)
+    finish(1)
+    value = finish(0)
+    for s in (2, 3, 1):
         arrived(s, BACK_Z)
         value = value + widen(z_in.at[s])
     out[...] = value.astype(out.dtype)
 
     def drain(s, carry):
-        sent(s, *range(OWN_X, BACK_Z))
+        sent(s, *range(OWN_XA, BACK_Z))
 
         @pl.when(s > 0)
         def _():
-            sent(s, BACK_Z, OUT_Z, META_Z)
+            sent(s, BACK_Z, META_Z)
 
         return carry
 
     lax.fori_loop(0, planes, drain, 0)
+    hop(0, 1).wait_send()
+
+    @at_middle
+    def _():
+        hop(0, 3).wait_send()
+        hop(1, 3).wait_send()
+        hop(2, 1).wait_send()
+        hop(3, 1).wait_send()
+
     for s in range(1, 4):
         sent(s, META_A)
     sent(0, META_C)

time: 77.9 us -> 72.6 us (0.932)
  the two profiles are of different devices: /device:TPU:9 before, /device:TPU:0 now
where the time goes in v1:
time: 72.6 us; the launch traced here: 72.5 us
  Pallas kernels  70.8 us (98%)
  local copies, waits for them, and re-layouts  1.61 us (2%)
    pallas_call x1, Pallas kernels, fused(): pl.pallas_call(kernel, out_shape=jax.ShapeDtypeStruct((rows, width), bf16...  70.8 us
    unnamed x1, local copies, waits for them, and re-layouts  1.61 us

profile of v1, /device:TPU:0, one launch (start us, length us, event | category | flops | bytes accessed | tf_op | source)
XLA Modules:
  0.0 72.5 jit_solution(6664075941744807752)
XLA Ops:
  0.0 70.8 %shard_map.82 = bf16[32,2880]{1,0:T(8,128)(2,1)} custom-call(bf16[32,2880]{1,0:T(8,128)(2,1)} %tokens.1, s32[4,32]{1,0:T(4,128)} %bitcast.6, f32[4,32]{1,0:T(4,128)} %bitcast.7, s32[8]{0:T(128)} %shed.1, s32[8]{0:T(128)} %partner.1, bf16[1,720,2880]{2,1,0:T(8,128)(2,1)} %bitcast.4, bf16[1,720,2880]{2,1,0:T(8,128)(2,1)} %bitcast.5, bf16[1,720,2880]{2,1,0:T(8,128)(2,1)} %down_hbm.1), custom_call_target="tpu_custom_call" | custom-call | tf_op jit(solution)/shard_map/pallas_call | solution.py:463
  70.9 1.6 %copy.10 = bf16[32,2880]{1,0:T(8,128)(2,1)} copy(bf16[32,2880]{1,0:T(8,128)(2,1)} %shard_map.82) | data formatting | bytes 368640

commit v2 on v1

--- a/solution.py
+++ b/solution.py
@@ -14,9 +14,10 @@
 MESH = pl.DeviceIdType.MESH
 
 OWN_XA, OWN_XB, OWN_YA, OWN_YB, OWN_C, FWD_Y, FWD_X, PASS_X, PASS_Y, PASS_D = range(10)
-SUM_C, HALF_X, HALF_Y, FULL_XA, FULL_XB, FULL_YA, FULL_YB, BACK_Z, OUT_Z = range(10, 19)
-META_Z, META_A, META_C = range(19, 22)
-KINDS = 22
+SUM_A, SUM_B, SUM_C, HALF_X, HALF_Y, FULL_XA, FULL_XB, FULL_YA, FULL_YB = range(10, 19)
+BACK_Z, OUT_Z, META_Z, META_A, META_C = range(19, 24)
+SUMS = (SUM_A, SUM_B, SUM_C)
+KINDS = 24
 
 
 def lookup(table, indices):
@@ -39,16 +40,19 @@
 
 def kernel(
     tokens,
-    ids,
-    probs,
-    shed,
-    partner,
+    ids_hbm,
+    probs_hbm,
+    shed_hbm,
+    partner_hbm,
     gate_hbm,
     up_hbm,
     down_hbm,
     out,
     x,
-    meta,
+    ids,
+    probs,
+    shed,
+    partner,
     m,
     wcol,
     part,
@@ -88,10 +92,16 @@
     oc = 1 - c
     to_x, to_y, to_d, to_c = (xn, e), (yn, e), (dn, e), (a, z * 2 + oc)
 
-    def plane(s):
+    def beyond(s):
         low = (z % 2 + s % 2) % 2
         high = (z // 2 + s // 2) % 2
         return high * 2 + low
+
+    def apart(k):
+        return k + middle * (k % 2) * (4 - 2 * k)
+
+    def plane(k):
+        return beyond(apart(k))
 
     def copy(kind, s, src, dst, to):
         return pltpu.make_async_remote_copy(
@@ -108,8 +118,17 @@
 
     lo, hi = pl.ds(0, half), pl.ds(half, half)
 
+    def chunks(size, step):
+        return [slice(first, min(first + step, size)) for first in range(0, size, step)]
+
+    lanes = -(-width // LANES)
+    wide = chunks(width, -(-lanes // len(SUMS)) * LANES)
+
     def make(kind, s):
-        p = plane(s)
+        if kind in (BACK_Z, META_Z):
+            away = (a, beyond(s) * 2 + c)
+        else:
+            p = plane(s)
         if kind == OWN_XA:
             return same(kind, s, x.at[p, c, a, lo], to_x)
         if kind == OWN_XB:
@@ -130,8 +149,10 @@
             return same(kind, s, x.at[p, c, yn], to_c)
         if kind == PASS_D:
             return same(kind, s, x.at[p, c, dn], to_c)
-        if kind == SUM_C:
-            return copy(kind, s, part.at[s, oc], core_in.at[s], to_c)
+        if kind in SUMS:
+            cols = wide[SUMS.index(kind)]
+            cols = pl.ds(cols.start, cols.stop - cols.start)
+            return copy(kind, s, part.at[s, oc, :, :, cols], core_in.at[s, :, :, cols], to_c)
         if kind == HALF_X:
             return copy(kind, s, total.at[s, dn, lo], half_in.at[s, 0], to_x)
         if kind == HALF_Y:
@@ -145,18 +166,18 @@
         if kind == FULL_YB:
             return copy(kind, s, total.at[s, yn, lo], full_in.at[s, 1, lo], to_y)
         if kind == BACK_Z:
-            return copy(kind, s, z_out.at[s], z_in.at[s], (a, p * 2 + c))
+            return copy(kind, s, z_out.at[s], z_in.at[s], away)
         if kind == META_Z:
-            return copy(kind, s, meta, m.at[a, z, c], (a, p * 2 + c))
+            return same(kind, s, m.at[:, z, c], away)
         if kind == META_A:
             to = (to_x, to_x, to_y, to_d)[s]
-            return same(kind, s, m.at[a, :, c], to)
+            return same(kind, s, m.at[a, z, c], to)
         if kind == META_C:
             return same(kind, s, m.at[:, :, c], to_c)
 
     def hop(block, target):
-        p = plane(block)
-        return same(OUT_Z, block ^ target, x.at[p, c, a], (a, plane(target) * 2 + c))
+        p = beyond(block)
+        return same(OUT_Z, block ^ target, x.at[p, c, a], (a, beyond(target) * 2 + c))
 
     def start(s, *kinds):
         for kind in kinds:
@@ -176,27 +197,34 @@
     def at_middle(run):
         pl.when(middle == 1)(run)
 
+    def at_end(run):
+        pl.when(middle == 0)(run)
+
     barrier = pltpu.get_barrier_semaphore()
-    peers = [to_x, to_y, to_d, to_c] + [(a, plane(s) * 2 + c) for s in range(1, planes)]
+    peers = [to_x, to_y, to_d, to_c] + [(a, beyond(s) * 2 + c) for s in range(1, planes)]
     for peer in peers:
         pl.semaphore_signal(barrier, inc=1, device_id=peer, device_id_type=MESH)
 
     own = pltpu.make_async_copy(tokens, x.at[z, c, a], load_sem.at[3])
-    own_meta = pltpu.make_async_copy(meta, m.at[a, z, c], load_sem.at[4])
+    small = [
+        pltpu.make_async_copy(ids_hbm, ids, load_sem.at[4]),
+        pltpu.make_async_copy(probs_hbm, probs, load_sem.at[5]),
+        pltpu.make_async_copy(shed_hbm, shed, load_sem.at[6]),
+        pltpu.make_async_copy(partner_hbm, partner, load_sem.at[7]),
+    ]
     loads = [
         pltpu.make_async_copy(gate_hbm.at[0], gate, load_sem.at[0]),
         pltpu.make_async_copy(up_hbm.at[0], up, load_sem.at[1]),
         pltpu.make_async_copy(down_hbm.at[0], down, load_sem.at[2]),
     ]
-    own.start()
-    meta[...] = jnp.full(meta.shape, -1.0, jnp.float32)
-    meta[:top, :rows] = ids[...].astype(jnp.float32)
-    meta[top:, :rows] = probs[...]
-    for load in loads:
+    for load in [own] + small + loads:
         load.start()
+    for load in small:
+        load.wait()
+    m[a, z, c] = jnp.full(m.shape[3:], -1.0, jnp.float32)
+    m[a, z, c, :top, :rows] = ids[...].astype(jnp.float32)
+    m[a, z, c, top:, :rows] = probs[...]
     own.wait()
-    own_meta.start()
-    own_meta.wait()
     pl.semaphore_wait(barrier, len(peers))
 
     def share_own(s):
@@ -222,21 +250,21 @@
         arrived(s, OWN_C, PASS_X, PASS_Y, PASS_D)
 
     def take(s):
-        hop(0, s).wait_recv()
+        same(OUT_Z, s, x.at[beyond(s), c, a], to_c).wait_recv()
 
     def out_1():
-        take(1)
+        take(apart(1))
 
         @at_middle
         def _():
-            hop(1, 3).start()
+            hop(3, 1).start()
 
         share_own(1)
 
         @at_middle
         def _():
-            take(3)
-            hop(3, 1).start()
+            take(1)
+            hop(1, 3).start()
 
     def out_2():
         take(2)
@@ -254,8 +282,8 @@
 
         share_own(3)
 
-    for s in range(1, planes):
-        start(s, META_Z)
+    for s in range(1, 4):
+        start(s, META_A)
     hop(0, 1).start()
 
     @at_middle
@@ -263,10 +291,10 @@
         hop(0, 3).start()
 
     share_own(0)
+    for s in range(1, 4):
+        arrived(s, META_A)
     for s in range(1, planes):
-        arrived(s, META_Z)
-    for s in range(1, 4):
-        start(s, META_A)
+        start(s, META_Z)
 
     def row_weights():
         table = m[...].reshape(m.shape[0] * m.shape[1] * m.shape[2], 2 * top, LANES)
@@ -312,16 +340,13 @@
             2, x.shape[2], rows, cols.stop - cols.start
         )
 
-    def chunks(size, step):
-        return [slice(first, min(first + step, size)) for first in range(0, size, step)]
-
     def core_sum(s, block, part_rows):
         return widen(part.at[s, c, block, part_rows]) + widen(core_in.at[s, block, part_rows])
 
     whole = pl.ds(0, rows)
 
     def begin(s):
-        arrived(s, SUM_C)
+        arrived(s, *SUMS)
         total[s, dn] = core_sum(s, dn, whole).astype(jnp.bfloat16)
         start(s, HALF_X, HALF_Y)
         total[s, xn, lo] = core_sum(s, xn, lo).astype(jnp.bfloat16)
@@ -345,12 +370,13 @@
         value = value + widen(full_in.at[s, 0]) + widen(full_in.at[s, 1])
         if s == 0:
             return value
-        z_out[s] = value.astype(jnp.bfloat16)
-        start(s, BACK_Z)
+        away = apart(s)
+        z_out[away] = value.astype(jnp.bfloat16)
+        start(away, BACK_Z)
 
     def get_meta():
-        for s in range(1, 4):
-            arrived(s, META_A)
+        for s in range(1, planes):
+            arrived(s, META_Z)
         start(0, META_C)
 
     def get_weights():
@@ -360,25 +386,28 @@
             load.wait()
 
     call = lambda run, s: lambda: run(s)
+    middle_does = lambda *runs: lambda: at_middle(lambda: [run() for run in runs] and None)
+    end_does = lambda *runs: lambda: at_end(lambda: [run() for run in runs] and None)
     before = [
-        call(forward, 0), get_meta, out_1, call(pass_near, 0), call(pass_far, 0), get_weights,
+        call(forward, 0), out_1, call(pass_near, 0), get_meta, call(pass_far, 0), get_weights,
         call(ready, 0),
     ]
     for run in before:
         run()
     hooks = {
         (0, 1): [call(forward, 1)],
-        (0, 4): [out_2],
-        (0, 5): [call(pass_near, 1)],
+        (0, 3): [out_2],
+        (0, 4): [call(pass_near, 1)],
         (1, 0): [call(pass_far, 1), call(ready, 1)],
         (1, 1): [call(forward, 2)],
         (1, 3): [out_3],
-        (1, 5): [call(pass_near, 2)],
+        (1, 4): [call(pass_near, 2)],
         (2, 0): [call(pass_far, 2), call(ready, 2)],
         (2, 1): [call(forward, 3), call(begin, 1)],
-        (2, 5): [call(pass_near, 3)],
-        (3, 0): [call(pass_far, 3), call(begin, 2), call(ready, 3)],
-        (3, 4): [call(merge, 2)],
+        (2, 4): [call(pass_near, 3)],
+        (3, 0): [call(pass_far, 3), call(ready, 3)],
+        (3, 1): [end_does(call(begin, 2))],
+        (3, 2): [middle_does(call(merge, 1), call(begin, 2))],
     }
 
     def hook(t, place):
@@ -398,22 +427,24 @@
             hook(t, place)
             hidden_piece(t, cols)
             place += 1
-        for cols in chunks(width, 8 * LANES):
+        for kind, cols in zip(SUMS, wide):
             hook(t, place)
             share_piece(t, cols)
+            start(t, kind)
             place += 1
-        start(t, SUM_C)
         return carry
 
     lax.fori_loop(0, planes, body, 0)
+    at_middle(lambda: finish(1))
+    merge(2)
     begin(3)
+    finish(2)
     merge(3)
-    merge(1)
+    at_end(lambda: merge(1))
     begin(0)
-    finish(2)
     finish(3)
+    at_end(lambda: finish(1))
     merge(0)
-    finish(1)
     value = finish(0)
     for s in (2, 3, 1):
         arrived(s, BACK_Z)
@@ -458,16 +489,18 @@
     table = (2 * ids.shape[0], LANES)
     bf16, f32 = jnp.bfloat16, jnp.float32
     vmem = pl.BlockSpec(memory_space=pltpu.VMEM)
-    smem = pl.BlockSpec(memory_space=pltpu.SMEM)
     hbm = pl.BlockSpec(memory_space=pl.ANY)
     return pl.pallas_call(
         kernel,
-        out_shape=jax.ShapeDtypeStruct((rows, width), bf16),
-        in_specs=[vmem, vmem, vmem, smem, smem, hbm, hbm, hbm],
+        out_shape=pltpu.VMEM((rows, width), bf16),
+        in_specs=[hbm] * 8,
         out_specs=vmem,
         scratch_shapes=[
             pltpu.VMEM((planes, 2, group_count, rows, width), bf16),
-            pltpu.VMEM(table, f32),
+            pltpu.VMEM(ids.shape, ids.dtype),
+            pltpu.VMEM(probs.shape, probs.dtype),
+            pltpu.SMEM(shed.shape, shed.dtype),
+            pltpu.SMEM(partner.shape, partner.dtype),
             pltpu.VMEM((group_count, planes, 2) + table, f32),
             pltpu.VMEM((planes, 2, group_count, rows, 1), f32),
             pltpu.VMEM((planes, 2, group_count, rows, width), bf16),
@@ -484,7 +517,7 @@
             pltpu.VMEM((count, hidden), bf16),
             pltpu.SemaphoreType.DMA((KINDS, planes)),
             pltpu.SemaphoreType.DMA((KINDS, planes)),
-            pltpu.SemaphoreType.DMA((5,)),
+            pltpu.SemaphoreType.DMA((8,)),
         ],
         compiler_params=pltpu.CompilerParams(
             collective_id=0, has_side_effects=True, vmem_limit_bytes=VMEM_BYTES

time: 72.6 us -> 67.1 us (0.924)
  Pallas kernels: 70.8 us -> 66.3 us
  local copies, waits for them, and re-layouts: 1.61 us -> 0.68 us
    pallas_call x1, Pallas kernels: 70.8 us -> 66.3 us  [fused(): pl.pallas_call(kernel, out_shape=pltpu.VMEM((rows, width), bf16), in_spec...]
    unnamed x1, local copies, waits for them, and re-layouts: 1.61 us -> 0.68 us
where the time goes in v2:
time: 67.1 us; the launch traced here: 67 us
  Pallas kernels  66.3 us (99%)
  local copies, waits for them, and re-layouts  0.68 us (1%)
    pallas_call x1, Pallas kernels, fused(): pl.pallas_call(kernel, out_shape=pltpu.VMEM((rows, width), bf16), in_spec...  66.3 us

profile of v2, /device:TPU:0, one launch (start us, length us, event | category | flops | bytes accessed | tf_op | source)
XLA Modules:
  0.0 67.0 jit_solution(16938754466339363451)
XLA Ops:
  0.0 66.3 %shard_map.82 = bf16[32,2880]{1,0:T(8,128)(2,1)S(1)} custom-call(bf16[32,2880]{1,0:T(8,128)(2,1)} %tokens.1, s32[4,32]{1,0:T(4,128)} %bitcast.6, f32[4,32]{1,0:T(4,128)} %bitcast.7, s32[8]{0:T(128)} %shed_hbm.1, s32[8]{0:T(128)} %partner_hbm.1, bf16[1,720,2880]{2,1,0:T(8,128)(2,1)} %bitcast.4, bf16[1,720,2880]{2,1,0:T(8,128)(2,1)} %bitcast.5, ...), custom_call_target="tpu_custom_call" | custom-call | tf_op jit(solution)/shard_map/pallas_call | solution.py:493
  66.3 0.7 %copy.10 = bf16[32,2880]{1,0:T(8,128)(2,1)} copy(bf16[32,2880]{1,0:T(8,128)(2,1)S(1)} %shard_map.82) | data formatting | bytes 368640

commit v3 on v2

--- a/solution.py
+++ b/solution.py
@@ -14,10 +14,14 @@
 MESH = pl.DeviceIdType.MESH
 
 OWN_XA, OWN_XB, OWN_YA, OWN_YB, OWN_C, FWD_Y, FWD_X, PASS_X, PASS_Y, PASS_D = range(10)
-SUM_A, SUM_B, SUM_C, HALF_X, HALF_Y, FULL_XA, FULL_XB, FULL_YA, FULL_YB = range(10, 19)
-BACK_Z, OUT_Z, META_Z, META_A, META_C = range(19, 24)
+SUM_A, SUM_B, SUM_C, OUT_Z, BACK_Z, META_Z, META_A = range(10, 17)
+HALF_X, HALF_Y, FULL_XA, FULL_XB, FULL_YA, FULL_YB, META_C = range(17, 24)
 SUMS = (SUM_A, SUM_B, SUM_C)
-KINDS = 24
+ROWS = 17
+ROW = {
+    HALF_X: OWN_XA, HALF_Y: OWN_YA, FULL_XA: OWN_XB, FULL_YA: OWN_YB, FULL_XB: FWD_X,
+    FULL_YB: FWD_Y, META_C: META_A,
+}
 
 
 def lookup(table, indices):
@@ -98,7 +102,7 @@
         return high * 2 + low
 
     def apart(k):
-        return k + middle * (k % 2) * (4 - 2 * k)
+        return k + middle * ((k + 1) % 3 + 1 - k) * ((k + 3) // 4)
 
     def plane(k):
         return beyond(apart(k))
@@ -107,8 +111,8 @@
         return pltpu.make_async_remote_copy(
             src_ref=src,
             dst_ref=dst,
-            send_sem=send_sem.at[kind, s],
-            recv_sem=recv_sem.at[kind, s],
+            send_sem=send_sem.at[0],
+            recv_sem=recv_sem.at[ROW.get(kind, kind), s],
             device_id=to,
             device_id_type=MESH,
         )
@@ -267,13 +271,12 @@
             hop(1, 3).start()
 
     def out_2():
+        at_end(lambda: take(2))
+        share_own(2)
+
+    def relay_2():
         take(2)
-
-        @at_middle
-        def _():
-            hop(2, 1).start()
-
-        share_own(2)
+        hop(2, 1).start()
 
     def out_3():
         @pl.when(middle == 0)
@@ -345,14 +348,20 @@
 
     whole = pl.ds(0, rows)
 
-    def begin(s):
+    def begin_half(s):
         arrived(s, *SUMS)
         total[s, dn] = core_sum(s, dn, whole).astype(jnp.bfloat16)
         start(s, HALF_X, HALF_Y)
+
+    def begin_full(s):
         total[s, xn, lo] = core_sum(s, xn, lo).astype(jnp.bfloat16)
         start(s, FULL_XA)
         total[s, yn, hi] = core_sum(s, yn, hi).astype(jnp.bfloat16)
         start(s, FULL_YA)
+
+    def begin(s):
+        begin_half(s)
+        begin_full(s)
 
     def merge(s):
         arrived(s, HALF_X)
@@ -396,18 +405,18 @@
         run()
     hooks = {
         (0, 1): [call(forward, 1)],
-        (0, 3): [out_2],
+        (0, 3): [out_2, middle_does(relay_2)],
         (0, 4): [call(pass_near, 1)],
-        (1, 0): [call(pass_far, 1), call(ready, 1)],
-        (1, 1): [call(forward, 2)],
-        (1, 3): [out_3],
-        (1, 4): [call(pass_near, 2)],
-        (2, 0): [call(pass_far, 2), call(ready, 2)],
-        (2, 1): [call(forward, 3), call(begin, 1)],
-        (2, 4): [call(pass_near, 3)],
-        (3, 0): [call(pass_far, 3), call(ready, 3)],
-        (3, 1): [end_does(call(begin, 2))],
-        (3, 2): [middle_does(call(merge, 1), call(begin, 2))],
+        (1, 0): [call(pass_far, 1), call(ready, 1), call(forward, 2)],
+        (1, 2): [out_3],
+        (1, 3): [call(pass_near, 2)],
+        (2, 0): [call(pass_far, 2), call(ready, 2), call(forward, 3)],
+        (2, 1): [call(begin, 1)],
+        (2, 3): [call(pass_near, 3)],
+        (3, 0): [
+            call(pass_far, 3), call(ready, 3), middle_does(call(merge, 1)), call(begin, 2),
+        ],
+        (3, 5): [end_does(call(merge, 2))],
     }
 
     def hook(t, place):
@@ -435,8 +444,7 @@
         return carry
 
     lax.fori_loop(0, planes, body, 0)
-    at_middle(lambda: finish(1))
-    merge(2)
+    at_middle(lambda: (finish(1), merge(2)) and None)
     begin(3)
     finish(2)
     merge(3)
@@ -452,7 +460,7 @@
     out[...] = value.astype(out.dtype)
 
     def drain(s, carry):
-        sent(s, *range(OWN_XA, BACK_Z))
+        sent(s, *range(OWN_XA, OUT_Z), *range(HALF_X, META_C))
 
         @pl.when(s > 0)
         def _():
@@ -515,8 +523,8 @@
             pltpu.VMEM((hidden, width), bf16),
             pltpu.VMEM((hidden, width), bf16),
             pltpu.VMEM((count, hidden), bf16),
-            pltpu.SemaphoreType.DMA((KINDS, planes)),
-            pltpu.SemaphoreType.DMA((KINDS, planes)),
+            pltpu.SemaphoreType.DMA((1,)),
+            pltpu.SemaphoreType.DMA((ROWS, planes)),
             pltpu.SemaphoreType.DMA((8,)),
         ],
         compiler_params=pltpu.CompilerParams(

time: 67.1 us -> 62.6 us (0.933)
  Pallas kernels: 66.3 us -> 61.7 us
    pallas_call x1, Pallas kernels: 66.3 us -> 61.7 us  [fused(): pl.pallas_call(kernel, out_shape=pltpu.VMEM((rows, width), bf16), in_spec...]
where the time goes in v3:
time: 62.6 us; the launch traced here: 62.4 us
  Pallas kernels  61.7 us (99%)
  local copies, waits for them, and re-layouts  0.68 us (1%)
    pallas_call x1, Pallas kernels, fused(): pl.pallas_call(kernel, out_shape=pltpu.VMEM((rows, width), bf16), in_spec...  61.7 us

profile of v3, /device:TPU:0, one launch (start us, length us, event | category | flops | bytes accessed | tf_op | source)
XLA Modules:
  0.0 62.4 jit_solution(5242385189972786849)
XLA Ops:
  0.0 61.7 %shard_map.82 = bf16[32,2880]{1,0:T(8,128)(2,1)S(1)} custom-call(bf16[32,2880]{1,0:T(8,128)(2,1)} %tokens.1, s32[4,32]{1,0:T(4,128)} %bitcast.6, f32[4,32]{1,0:T(4,128)} %bitcast.7, s32[8]{0:T(128)} %shed_hbm.1, s32[8]{0:T(128)} %partner_hbm.1, bf16[1,720,2880]{2,1,0:T(8,128)(2,1)} %bitcast.4, bf16[1,720,2880]{2,1,0:T(8,128)(2,1)} %bitcast.5, ...), custom_call_target="tpu_custom_call" | custom-call | tf_op jit(solution)/shard_map/pallas_call | solution.py:501
  61.7 0.7 %copy.10 = bf16[32,2880]{1,0:T(8,128)(2,1)} copy(bf16[32,2880]{1,0:T(8,128)(2,1)S(1)} %shard_map.82) | data formatting | bytes 368640

commit v4 on v3

--- a/solution.py
+++ b/solution.py
@@ -14,13 +14,17 @@
 MESH = pl.DeviceIdType.MESH
 
 OWN_XA, OWN_XB, OWN_YA, OWN_YB, OWN_C, FWD_Y, FWD_X, PASS_X, PASS_Y, PASS_D = range(10)
-SUM_A, SUM_B, SUM_C, OUT_Z, BACK_Z, META_Z, META_A = range(10, 17)
-HALF_X, HALF_Y, FULL_XA, FULL_XB, FULL_YA, FULL_YB, META_C = range(17, 24)
-SUMS = (SUM_A, SUM_B, SUM_C)
-ROWS = 17
+SUM_A, SUM_B, OUT_Z, BACK_Z, META_Z, META_A, LATE_X, LATE_Y, LATE_Z = range(10, 19)
+ROWS = 19
+HALF_X, HALF_Y, FULL_XA, FULL_XB, FULL_YA, FULL_YB, META_C, DIAG_Z = range(19, 27)
+SUMS = (SUM_A, SUM_B)
 ROW = {
     HALF_X: OWN_XA, HALF_Y: OWN_YA, FULL_XA: OWN_XB, FULL_YA: OWN_YB, FULL_XB: FWD_X,
-    FULL_YB: FWD_Y, META_C: META_A,
+    FULL_YB: FWD_Y, META_C: META_A, DIAG_Z: META_Z,
+}
+LATE_ROW = {
+    HALF_X: PASS_X, HALF_Y: PASS_Y, FULL_XA: PASS_D, FULL_YA: OWN_C, FULL_XB: LATE_X,
+    FULL_YB: LATE_Y, BACK_Z: LATE_Z, DIAG_Z: LATE_Z,
 }
 
 
@@ -66,7 +70,7 @@
     full_in,
     z_out,
     z_in,
-    kept,
+    diag_in,
     gate,
     up,
     down,
@@ -102,17 +106,19 @@
         return high * 2 + low
 
     def apart(k):
-        return k + middle * ((k + 1) % 3 + 1 - k) * ((k + 3) // 4)
+        inner = ((k + 1) % 3 + 1 - k) * ((k + 3) // 4)
+        return k + middle * (inner + (z // 2) * (k // 2) * (5 - 2 * k))
 
     def plane(k):
         return beyond(apart(k))
 
-    def copy(kind, s, src, dst, to):
+    def copy(kind, s, src, dst, to, late=0):
+        row = LATE_ROW[kind] if late else ROW.get(kind, kind)
         return pltpu.make_async_remote_copy(
             src_ref=src,
             dst_ref=dst,
             send_sem=send_sem.at[0],
-            recv_sem=recv_sem.at[ROW.get(kind, kind), s],
+            recv_sem=recv_sem.at[row, s],
             device_id=to,
             device_id_type=MESH,
         )
@@ -128,7 +134,8 @@
     lanes = -(-width // LANES)
     wide = chunks(width, -(-lanes // len(SUMS)) * LANES)
 
-    def make(kind, s):
+    def make(kind, s, q=0):
+        cols = pl.ds(wide[q].start, wide[q].stop - wide[q].start)
         if kind in (BACK_Z, META_Z):
             away = (a, beyond(s) * 2 + c)
         else:
@@ -157,20 +164,23 @@
             cols = wide[SUMS.index(kind)]
             cols = pl.ds(cols.start, cols.stop - cols.start)
             return copy(kind, s, part.at[s, oc, :, :, cols], core_in.at[s, :, :, cols], to_c)
+        if kind == DIAG_Z:
+            to = (a, beyond(1) * 2 + c)
+            return copy(kind, 0, total.at[s, dn, :, cols], diag_in.at[:, cols], to, q)
         if kind == HALF_X:
-            return copy(kind, s, total.at[s, dn, lo], half_in.at[s, 0], to_x)
+            return copy(kind, s, total.at[s, dn, lo, cols], half_in.at[s, 0, :, cols], to_x, q)
         if kind == HALF_Y:
-            return copy(kind, s, total.at[s, dn, hi], half_in.at[s, 1], to_y)
+            return copy(kind, s, total.at[s, dn, hi, cols], half_in.at[s, 1, :, cols], to_y, q)
         if kind == FULL_XA:
-            return copy(kind, s, total.at[s, xn, lo], full_in.at[s, 0, lo], to_x)
+            return copy(kind, s, total.at[s, xn, lo, cols], full_in.at[s, 0, lo, cols], to_x, q)
         if kind == FULL_XB:
-            return copy(kind, s, total.at[s, xn, hi], full_in.at[s, 0, hi], to_x)
+            return copy(kind, s, total.at[s, xn, hi, cols], full_in.at[s, 0, hi, cols], to_x, q)
         if kind == FULL_YA:
-            return copy(kind, s, total.at[s, yn, hi], full_in.at[s, 1, hi], to_y)
+            return copy(kind, s, total.at[s, yn, hi, cols], full_in.at[s, 1, hi, cols], to_y, q)
         if kind == FULL_YB:
-            return copy(kind, s, total.at[s, yn, lo], full_in.at[s, 1, lo], to_y)
+            return copy(kind, s, total.at[s, yn, lo, cols], full_in.at[s, 1, lo, cols], to_y, q)
         if kind == BACK_Z:
-            return copy(kind, s, z_out.at[s], z_in.at[s], away)
+            return copy(kind, s, z_out.at[s, :, cols], z_in.at[s, :, cols], away, q)
         if kind == META_Z:
             return same(kind, s, m.at[:, z, c], away)
         if kind == META_A:
@@ -183,17 +193,17 @@
         p = beyond(block)
         return same(OUT_Z, block ^ target, x.at[p, c, a], (a, beyond(target) * 2 + c))
 
-    def start(s, *kinds):
+    def start(s, *kinds, q=0):
         for kind in kinds:
-            make(kind, s).start()
-
-    def arrived(s, *kinds):
+            make(kind, s, q).start()
+
+    def arrived(s, *kinds, q=0):
         for kind in kinds:
-            make(kind, s).wait_recv()
-
-    def sent(s, *kinds):
+            make(kind, s, q).wait_recv()
+
+    def sent(s, *kinds, q=0):
         for kind in kinds:
-            make(kind, s).wait_send()
+            make(kind, s, q).wait_send()
 
     def widen(ref):
         return ref[...].astype(jnp.float32)
@@ -271,12 +281,14 @@
             hop(1, 3).start()
 
     def out_2():
+        def relay_2():
+            take(2)
+            hop(2, 1).start()
+
         at_end(lambda: take(2))
+        pl.when(z == 2)(relay_2)
         share_own(2)
-
-    def relay_2():
-        take(2)
-        hop(2, 1).start()
+        pl.when(z == 1)(relay_2)
 
     def out_3():
         @pl.when(middle == 0)
@@ -343,45 +355,85 @@
             2, x.shape[2], rows, cols.stop - cols.start
         )
 
-    def core_sum(s, block, part_rows):
-        return widen(part.at[s, c, block, part_rows]) + widen(core_in.at[s, block, part_rows])
+    def core_sum(s, block, part_rows, q):
+        cols = wide[q]
+        return widen(part.at[s, c, block, part_rows, cols]) + widen(
+            core_in.at[s, block, part_rows, cols]
+        )
 
     whole = pl.ds(0, rows)
 
-    def begin_half(s):
-        arrived(s, *SUMS)
-        total[s, dn] = core_sum(s, dn, whole).astype(jnp.bfloat16)
-        start(s, HALF_X, HALF_Y)
-
-    def begin_full(s):
-        total[s, xn, lo] = core_sum(s, xn, lo).astype(jnp.bfloat16)
-        start(s, FULL_XA)
-        total[s, yn, hi] = core_sum(s, yn, hi).astype(jnp.bfloat16)
-        start(s, FULL_YA)
+    def either(s, diagonal, plain):
+        if s == 0:
+            plain()
+        elif s == 1:
+            at_end(diagonal)
+            at_middle(plain)
+        else:
+            pl.when(z == s - 1)(diagonal)
+            pl.when(z != s - 1)(plain)
+
+    def begin_half(s, q):
+        cols = wide[q]
+        arrived(s, SUMS[q])
+        far = core_sum(s, dn, whole, q)
+        if s == 0:
+            arrived(0, DIAG_Z, q=q)
+            far = far + widen(diag_in.at[:, cols])
+        total[s, dn, :, cols] = far.astype(jnp.bfloat16)
+        either(s, lambda: start(s, DIAG_Z, q=q), lambda: start(s, HALF_X, HALF_Y, q=q))
+
+    def begin_full(s, q):
+        cols = wide[q]
+        total[s, xn, lo, cols] = core_sum(s, xn, lo, q).astype(jnp.bfloat16)
+        start(s, FULL_XA, q=q)
+        total[s, yn, hi, cols] = core_sum(s, yn, hi, q).astype(jnp.bfloat16)
+        start(s, FULL_YA, q=q)
+
+        def diagonal():
+            total[s, yn, lo, cols] = core_sum(s, yn, lo, q).astype(jnp.bfloat16)
+            start(s, FULL_YB, q=q)
+            total[s, xn, hi, cols] = core_sum(s, xn, hi, q).astype(jnp.bfloat16)
+            start(s, FULL_XB, q=q)
+
+        either(s, diagonal, lambda: None)
 
     def begin(s):
-        begin_half(s)
-        begin_full(s)
-
-    def merge(s):
-        arrived(s, HALF_X)
-        low = core_sum(s, yn, lo) + widen(half_in.at[s, 0])
-        total[s, yn, lo] = low.astype(jnp.bfloat16)
-        start(s, FULL_YB)
-        arrived(s, HALF_Y)
-        high = core_sum(s, xn, hi) + widen(half_in.at[s, 1])
-        total[s, xn, hi] = high.astype(jnp.bfloat16)
-        start(s, FULL_XB)
-
-    def finish(s):
-        value = core_sum(s, a, whole)
-        arrived(s, FULL_XA, FULL_YA, FULL_XB, FULL_YB)
-        value = value + widen(full_in.at[s, 0]) + widen(full_in.at[s, 1])
-        if s == 0:
-            return value
-        away = apart(s)
-        z_out[away] = value.astype(jnp.bfloat16)
-        start(away, BACK_Z)
+        begin_half(s, 0)
+        begin_full(s, 0)
+        begin_half(s, 1)
+        begin_full(s, 1)
+
+    def merge(s, *pieces):
+        def plain():
+            for q in pieces or (0, 1):
+                cols = wide[q]
+                arrived(s, HALF_X, q=q)
+                low = core_sum(s, yn, lo, q) + widen(half_in.at[s, 0, :, cols])
+                total[s, yn, lo, cols] = low.astype(jnp.bfloat16)
+                start(s, FULL_YB, q=q)
+                arrived(s, HALF_Y, q=q)
+                high = core_sum(s, xn, hi, q) + widen(half_in.at[s, 1, :, cols])
+                total[s, xn, hi, cols] = high.astype(jnp.bfloat16)
+                start(s, FULL_XB, q=q)
+
+        either(s, lambda: None, plain)
+
+    def finish(s, *pieces):
+        for q in pieces or (0, 1):
+            cols = wide[q]
+            value = core_sum(s, a, whole, q)
+            arrived(s, FULL_XA, FULL_YA, FULL_XB, FULL_YB, q=q)
+            value = value + widen(full_in.at[s, 0, :, cols]) + widen(full_in.at[s, 1, :, cols])
+            if s == 0:
+                for far in (2, 3, 1):
+                    arrived(far, BACK_Z, q=q)
+                    value = value + widen(z_in.at[far, :, cols])
+                out[:, cols] = value.astype(out.dtype)
+            else:
+                away = apart(s)
+                z_out[away, :, cols] = value.astype(jnp.bfloat16)
+                start(away, BACK_Z, q=q)
 
     def get_meta():
         for s in range(1, planes):
@@ -405,7 +457,7 @@
         run()
     hooks = {
         (0, 1): [call(forward, 1)],
-        (0, 3): [out_2, middle_does(relay_2)],
+        (0, 3): [out_2],
         (0, 4): [call(pass_near, 1)],
         (1, 0): [call(pass_far, 1), call(ready, 1), call(forward, 2)],
         (1, 2): [out_3],
@@ -416,7 +468,7 @@
         (3, 0): [
             call(pass_far, 3), call(ready, 3), middle_does(call(merge, 1)), call(begin, 2),
         ],
-        (3, 5): [end_does(call(merge, 2))],
+        (3, 4): [end_does(lambda: merge(2, 0))],
     }
 
     def hook(t, place):
@@ -444,27 +496,37 @@
         return carry
 
     lax.fori_loop(0, planes, body, 0)
-    at_middle(lambda: (finish(1), merge(2)) and None)
-    begin(3)
+    finish(1)
+    at_end(lambda: merge(2, 1))
+    pl.when(z == 2)(lambda: merge(2))
+    begin_half(3, 0)
+    begin_full(3, 0)
+    begin_half(3, 1)
     finish(2)
-    merge(3)
-    at_end(lambda: merge(1))
+    merge(3, 0)
+    begin_full(3, 1)
+    merge(3, 1)
+
+    def finish_3():
+        finish(3, 0)
+        finish(3, 1)
+
+    pl.when(z == planes - 1)(finish_3)
     begin(0)
-    finish(3)
-    at_end(lambda: finish(1))
+    pl.when(z != planes - 1)(finish_3)
     merge(0)
-    value = finish(0)
-    for s in (2, 3, 1):
-        arrived(s, BACK_Z)
-        value = value + widen(z_in.at[s])
-    out[...] = value.astype(out.dtype)
+    finish(0)
 
     def drain(s, carry):
-        sent(s, *range(OWN_XA, OUT_Z), *range(HALF_X, META_C))
+        sent(s, *range(OWN_XA, OUT_Z))
+        for q in range(len(SUMS)):
+            sent(s, *range(HALF_X, META_C), q=q)
 
         @pl.when(s > 0)
         def _():
-            sent(s, BACK_Z, META_Z)
+            sent(s, META_Z)
+            for q in range(len(SUMS)):
+                sent(s, BACK_Z, q=q)
 
         return carry
 
@@ -518,7 +580,7 @@
             pltpu.VMEM((planes, 2, rows, width), bf16),
             pltpu.VMEM((planes, rows, width), bf16),
             pltpu.VMEM((planes, rows, width), bf16),
-            pltpu.VMEM((rows, width), f32),
+            pltpu.VMEM((rows, width), bf16),
             pltpu.VMEM((hidden, width), bf16),
             pltpu.VMEM((hidden, width), bf16),
             pltpu.VMEM((hidden, width), bf16),

time: 62.6 us -> 61.2 us (0.978)
  Pallas kernels: 61.7 us -> 60.3 us
    pallas_call x1, Pallas kernels: 61.7 us -> 60.3 us  [fused(): pl.pallas_call(kernel, out_shape=pltpu.VMEM((rows, width), bf16), in_spec...]
where the time goes in v4:
time: 61.2 us; the launch traced here: 61 us
  Pallas kernels  60.3 us (99%)
  local copies, waits for them, and re-layouts  0.68 us (1%)
    pallas_call x1, Pallas kernels, fused(): pl.pallas_call(kernel, out_shape=pltpu.VMEM((rows, width), bf16), in_spec...  60.3 us

profile of v4, /device:TPU:0, one launch (start us, length us, event | category | flops | bytes accessed | tf_op | source)
XLA Modules:
  0.0 61.0 jit_solution(17280671547180901312)
XLA Ops:
  0.0 60.3 %shard_map.82 = bf16[32,2880]{1,0:T(8,128)(2,1)S(1)} custom-call(bf16[32,2880]{1,0:T(8,128)(2,1)} %tokens.1, s32[4,32]{1,0:T(4,128)} %bitcast.6, f32[4,32]{1,0:T(4,128)} %bitcast.7, s32[8]{0:T(128)} %shed_hbm.1, s32[8]{0:T(128)} %partner_hbm.1, bf16[1,720,2880]{2,1,0:T(8,128)(2,1)} %bitcast.4, bf16[1,720,2880]{2,1,0:T(8,128)(2,1)} %bitcast.5, ...), custom_call_target="tpu_custom_call" | custom-call | tf_op jit(solution)/shard_map/pallas_call | solution.py:563
  60.3 0.7 %copy.10 = bf16[32,2880]{1,0:T(8,128)(2,1)} copy(bf16[32,2880]{1,0:T(8,128)(2,1)S(1)} %shard_map.82) | data formatting | bytes 368640

commit v5 on v4

--- a/solution.py
+++ b/solution.py
@@ -16,11 +16,11 @@
 OWN_XA, OWN_XB, OWN_YA, OWN_YB, OWN_C, FWD_Y, FWD_X, PASS_X, PASS_Y, PASS_D = range(10)
 SUM_A, SUM_B, OUT_Z, BACK_Z, META_Z, META_A, LATE_X, LATE_Y, LATE_Z = range(10, 19)
 ROWS = 19
-HALF_X, HALF_Y, FULL_XA, FULL_XB, FULL_YA, FULL_YB, META_C, DIAG_Z = range(19, 27)
+HALF_X, HALF_Y, FULL_XA, FULL_XB, FULL_YA, FULL_YB, META_C, DIAG_Z, FEED_Z = range(19, 28)
 SUMS = (SUM_A, SUM_B)
 ROW = {
     HALF_X: OWN_XA, HALF_Y: OWN_YA, FULL_XA: OWN_XB, FULL_YA: OWN_YB, FULL_XB: FWD_X,
-    FULL_YB: FWD_Y, META_C: META_A, DIAG_Z: META_Z,
+    FULL_YB: FWD_Y, META_C: META_A, DIAG_Z: META_Z, FEED_Z: OUT_Z,
 }
 LATE_ROW = {
     HALF_X: PASS_X, HALF_Y: PASS_Y, FULL_XA: PASS_D, FULL_YA: OWN_C, FULL_XB: LATE_X,
@@ -164,6 +164,8 @@
             cols = wide[SUMS.index(kind)]
             cols = pl.ds(cols.start, cols.stop - cols.start)
             return copy(kind, s, part.at[s, oc, :, :, cols], core_in.at[s, :, :, cols], to_c)
+        if kind == FEED_Z:
+            return same(kind, 0, x.at[beyond(s), c, dn], (a, beyond(1) * 2 + c))
         if kind == DIAG_Z:
             to = (a, beyond(1) * 2 + c)
             return copy(kind, 0, total.at[s, dn, :, cols], diag_in.at[:, cols], to, q)
@@ -244,11 +246,21 @@
     def share_own(s):
         start(s, OWN_XA, OWN_YA, OWN_XB, OWN_YB, OWN_C)
 
+    def unfed(s, run):
+        if s < 2:
+            run()
+        else:
+            pl.when(z != s - 1)(run)
+
+    def fed(s, run):
+        if s >= 2:
+            pl.when(z == s - 1)(run)
+
     def forward(s):
         arrived(s, OWN_XA)
-        start(s, FWD_Y)
+        unfed(s, lambda: start(s, FWD_Y))
         arrived(s, OWN_YA)
-        start(s, FWD_X)
+        unfed(s, lambda: start(s, FWD_X))
 
     def pass_near(s):
         arrived(s, OWN_XB)
@@ -257,8 +269,20 @@
         start(s, PASS_Y)
 
     def pass_far(s):
-        arrived(s, FWD_Y, FWD_X)
-        start(s, PASS_D)
+        def plain():
+            arrived(s, FWD_Y, FWD_X)
+            start(s, PASS_D)
+
+        unfed(s, plain)
+        if s == 0:
+            at_end(lambda: start(0, FEED_Z))
+
+    def pass_fed(s):
+        def near():
+            arrived(1, FEED_Z)
+            start(s, PASS_D)
+
+        fed(s, near)
 
     def ready(s):
         arrived(s, OWN_C, PASS_X, PASS_Y, PASS_D)
@@ -400,8 +424,8 @@
 
     def begin(s):
         begin_half(s, 0)
+        begin_half(s, 1)
         begin_full(s, 0)
-        begin_half(s, 1)
         begin_full(s, 1)
 
     def merge(s, *pieces):
@@ -461,13 +485,14 @@
         (0, 4): [call(pass_near, 1)],
         (1, 0): [call(pass_far, 1), call(ready, 1), call(forward, 2)],
         (1, 2): [out_3],
-        (1, 3): [call(pass_near, 2)],
-        (2, 0): [call(pass_far, 2), call(ready, 2), call(forward, 3)],
+        (1, 3): [call(pass_near, 2), call(pass_fed, 2)],
+        (2, 0): [call(pass_far, 2), call(ready, 2), lambda: unfed(3, lambda: forward(3))],
         (2, 1): [call(begin, 1)],
-        (2, 3): [call(pass_near, 3)],
+        (2, 3): [lambda: fed(3, lambda: forward(3)), call(pass_near, 3), call(pass_fed, 3)],
         (3, 0): [
-            call(pass_far, 3), call(ready, 3), middle_does(call(merge, 1)), call(begin, 2),
+            middle_does(call(merge, 1)), call(pass_far, 3), call(ready, 3), call(begin, 2),
         ],
+        (3, 2): [middle_does(call(finish, 1))],
         (3, 4): [end_does(lambda: merge(2, 0))],
     }
 
@@ -496,13 +521,14 @@
         return carry
 
     lax.fori_loop(0, planes, body, 0)
-    finish(1)
+    at_end(lambda: finish(1))
     at_end(lambda: merge(2, 1))
     pl.when(z == 2)(lambda: merge(2))
     begin_half(3, 0)
     begin_full(3, 0)
+    pl.when(z == 1)(lambda: finish(2))
     begin_half(3, 1)
-    finish(2)
+    pl.when(z != 1)(lambda: finish(2))
     merge(3, 0)
     begin_full(3, 1)
     merge(3, 1)
@@ -518,7 +544,12 @@
     finish(0)
 
     def drain(s, carry):
-        sent(s, *range(OWN_XA, OUT_Z))
+        sent(s, *range(OWN_XA, FWD_Y), *range(PASS_X, OUT_Z))
+
+        @pl.when(jnp.logical_or(middle == 0, apart(s) != 1))
+        def _():
+            sent(s, FWD_Y, FWD_X)
+
         for q in range(len(SUMS)):
             sent(s, *range(HALF_X, META_C), q=q)
 
@@ -531,6 +562,7 @@
         return carry
 
     lax.fori_loop(0, planes, drain, 0)
+    at_end(lambda: sent(0, FEED_Z))
     hop(0, 1).wait_send()
 
     @at_middle

time: 61.2 us -> 60.3 us (0.985); the launches traced: 61 us -> 59.4 us
  Pallas kernels: 60.3 us -> 58.7 us
    pallas_call x1, Pallas kernels: 60.3 us -> 58.7 us  [fused(): pl.pallas_call(kernel, out_shape=pltpu.VMEM((rows, width), bf16), in_spec...]
where the time goes in v5:
time: 60.3 us; the launch traced here: 59.4 us
  Pallas kernels  58.7 us (97%)
  local copies, waits for them, and re-layouts  0.68 us (1%)
    pallas_call x1, Pallas kernels, fused(): pl.pallas_call(kernel, out_shape=pltpu.VMEM((rows, width), bf16), in_spec...  58.7 us

profile of v5, /device:TPU:0, one launch (start us, length us, event | category | flops | bytes accessed | tf_op | source)
XLA Modules:
  0.0 59.4 jit_solution(10794225530897937061)
XLA Ops:
  0.0 58.7 %shard_map.82 = bf16[32,2880]{1,0:T(8,128)(2,1)S(1)} custom-call(bf16[32,2880]{1,0:T(8,128)(2,1)} %tokens.1, s32[4,32]{1,0:T(4,128)} %bitcast.6, f32[4,32]{1,0:T(4,128)} %bitcast.7, s32[8]{0:T(128)} %shed_hbm.1, s32[8]{0:T(128)} %partner_hbm.1, bf16[1,720,2880]{2,1,0:T(8,128)(2,1)} %bitcast.4, bf16[1,720,2880]{2,1,0:T(8,128)(2,1)} %bitcast.5, ...), custom_call_target="tpu_custom_call" | custom-call | tf_op jit(solution)/shard_map/pallas_call | solution.py:595
  58.7 0.7 %copy.10 = bf16[32,2880]{1,0:T(8,128)(2,1)} copy(bf16[32,2880]{1,0:T(8,128)(2,1)S(1)} %shard_map.82) | data formatting | bytes 368640
